TPU v7x, 32 devices: a whole 2x2x4 slice. The times are simulated.
32 devices in a mesh: seq: 8 (over z, x), head: 4 (over y, core).
Axes of the slice: x: 2, y: 2, z: 4, core: 2. Of those that a mesh axis runs over, the one named last changes fastest.
Arguments:
- queries: bfloat16 [4096, 4096], P('seq', 'head'), may hold values from -120 to 120
- keys: bfloat16 [4096, 1024], P('seq', 'head'), may hold values from -4 to 4
- values: bfloat16 [4096, 1024], P('seq', 'head'), may hold values from -6 to 6
- doc_start: int32 [4096], P('seq'), may hold values from 0 to 4095, as said below
- hop_counts: int32 [8], P('seq'), may hold values from 0 to 4, as said below
- loss_mask: int32 [4096], P('seq'), may hold values from 0 to 1, as said below
Outputs:
- attention: bfloat16 [4096, 4096], P('seq', 'head')
- objective: float32 [], replicated
Inputs may be any that keep to these rules, and one draw needn't show every extreme that they name: doc_start is nondecreasing; doc_start[doc_start[i]] = doc_start[i] <= i; a document holds at most 2048 tokens, and some document holds exactly that many in every draw. hop_counts[b] = b - floor(doc_start[b * 512] / 512); the most, 4, is reached in every draw. loss_mask[0] = 1.
All inputs are finite; a program needn't handle non-finite values.
Results may differ from a plain program's by a relative error of at most 0.0035.
Values may be sent and summed in bfloat16 or wider, within the bound.
A program may use at most 128 MiB of HBM per device.

v0:
```python
import math

import jax
import jax.numpy as jnp
from jax import lax
from jax.sharding import PartitionSpec as P

QUERY_HEADS = 32
KEY_VALUE_HEADS = 8
HEAD_WIDTH = 128
HOPS = 4


def passed_along(shard, axis, by):
    devices = lax.axis_size(axis)
    pairs = [(i, i + by) for i in range(devices) if 0 <= i + by < devices]
    return lax.ppermute(shard, axis, pairs)


def attend_block(
    carry, key_block, value_block, distance, grouped_queries, doc_start, block_index, hop_limit
):
    top_old, total_old, weighted = carry
    rows = grouped_queries.shape[0]
    scores = jnp.einsum(
        "tgqd,sgd->tgqs", grouped_queries, key_block, preferred_element_type=jnp.float32
    ) * (1.0 / math.sqrt(HEAD_WIDTH))
    key_place = (block_index - distance) * rows + jnp.arange(rows, dtype=jnp.int32)
    query_place = block_index * rows + jnp.arange(rows, dtype=jnp.int32)
    seen = (
        (key_place[None, :] >= doc_start[:, None])
        & (key_place[None, :] <= query_place[:, None])
        & (distance <= hop_limit)
    )
    seen = seen[:, None, None, :]
    masked = jnp.where(seen, scores, jnp.float32(-1e30))
    top_new = jnp.maximum(top_old, jnp.max(masked, axis=-1))
    ratio_old = jnp.exp(top_old - top_new)
    weights = jnp.where(seen, jnp.exp(masked - top_new[..., None]), jnp.float32(0.0))
    total_new = total_old * ratio_old + jnp.sum(weights, axis=-1)
    rounded = weights.astype(jnp.bfloat16)
    update = jnp.einsum("tgqs,sgd->tgqd", rounded, value_block, preferred_element_type=jnp.float32)
    return (top_new, total_new, weighted * ratio_old[..., None] + update)


def on_device(queries, keys, values, doc_start, hop_counts, loss_mask):
    rows = queries.shape[0]
    kv_heads = keys.shape[1] // HEAD_WIDTH
    group_size = QUERY_HEADS // KEY_VALUE_HEADS
    block_index = lax.axis_index("seq")
    hop_limit = hop_counts[0]
    grouped_queries = queries.reshape(rows, kv_heads, group_size, HEAD_WIDTH)
    carry = (
        jnp.full((rows, kv_heads, group_size), -1e30, jnp.float32),
        jnp.zeros((rows, kv_heads, group_size), jnp.float32),
        jnp.zeros((rows, kv_heads, group_size, HEAD_WIDTH), jnp.float32),
    )

    def absorb(state, key_part, value_part, distance):
        key_block = key_part.reshape(rows, kv_heads, HEAD_WIDTH)
        value_block = value_part.reshape(rows, kv_heads, HEAD_WIDTH)
        return attend_block(
            state,
            key_block,
            value_block,
            distance,
            grouped_queries,
            doc_start,
            block_index,
            hop_limit,
        )

    carry = absorb(carry, keys, values, 0)
    moving_keys, moving_values = (keys, values)
    for distance in range(1, HOPS + 1):
        moving_keys, moving_values = passed_along((moving_keys, moving_values), "seq", 1)
        carry = absorb(carry, moving_keys, moving_values, distance)
    top_final, total_final, weighted = carry
    attended = (weighted / total_final[..., None]).reshape(rows, kv_heads * group_size * HEAD_WIDTH)
    attention = attended.astype(jnp.bfloat16)
    marks = loss_mask.astype(jnp.float32)
    local_squares = jnp.sum(marks[:, None] * attended * attended)
    local_count = jnp.sum(marks)
    head_index = lax.axis_index("head")
    share = jnp.where(head_index == 0, local_count, jnp.float32(0.0))
    squares_total, count_total = lax.psum((local_squares, share), ("seq", "head"))
    objective = squares_total / (QUERY_HEADS * count_total)
    return (attention, objective)


def solution(mesh):
    placed = (P("seq", "head"), P("seq", "head"), P("seq", "head"), P("seq"), P("seq"), P("seq"))
    return jax.shard_map(
        on_device, mesh=mesh, in_specs=placed, out_specs=(P("seq", "head"), P()), check_vma=False
    )
```

profile of v0, /device:TPU:0, one launch (start us, length us, event | category | flops | bytes accessed | tf_op | source)
XLA Modules:
  0.0 152.4 jit_solution(7085627525327538514)
XLA Ops:
  0.6 1.1 copy.29
  1.7 4.9 %collective-permute-start = (bf16[512,256]{0,1:T(8,128)(2,1)S(1)}, bf16[512,256]{0,1:T(8,128)(2,1)S(1)}, u32[]{:S(2)}, u32[]{:S(2)}) collective-permute-start(bf16[512,256]{0,1:T(8,128)(2,1)S(1)} %copy.29), channel_id=1, source_target_pairs={{0,4},{4,8},{8,12},{12,16},{16,20},{20,24},{24,28},{1,5},{5,9},{9,... | collective-permute-start | bytes 786440 | tf_op jit(solution)/shard_map/ppermute | solution.py:17
  6.6 3.5 %collective-permute-start.1 = (bf16[512,256]{1,0:T(8,128)(2,1)}, bf16[512,256]{1,0:T(8,128)(2,1)S(1)}, u32[]{:S(2)}, u32[]{:S(2)}) collective-permute-start(bf16[512,256]{1,0:T(8,128)(2,1)} %param.8), channel_id=1, source_target_pairs={{0,4},{4,8},{8,12},{12,16},{16,20},{20,24},{24,28},{1,5},{5,9},{9,... | collective-permute-start | bytes 786440 | tf_op jit(solution)/shard_map/ppermute | solution.py:17
  10.1 1.7 %reshape.416 = bf16[512,2,128]{2,1,0:T(2,128)(2,1)} reshape(bf16[512,256]{1,0:T(8,128)(2,1)} %param.7) | data formatting | bytes 524288 | tf_op jit(solution)/shard_map/reshape | solution.py:60
  11.8 1.1 copy.64
  12.9 0.7 convert_element_type.31
  13.6 1.3 convert_reduce_fusion
  15.6 1.8 %reshape.417 = bf16[512,2,4,128]{3,2,1,0:T(4,128)(2,1)S(1)} reshape(bf16[512,1024]{1,0:T(8,128)(2,1)} %param.6) | data formatting | bytes 2097152 | tf_op jit(solution)/shard_map/reshape | solution.py:52
  18.1 2.1 %and_and_fusion.4 = (pred[512,512]{0,1:T(8,128)(4,1)S(1)}, pred[512,512]{0,1:T(8,128)(4,1)S(1)}, pred[512,512]{0,1:T(8,128)(4,1)S(1)}, pred[512,512]{0,1:T(8,128)(4,1)S(1)}, pred[512,512]{0,1:T(8,128)(4,1)S(1)}) fusion(s32[512]{0:T(512)S(1)} %iota_add_fusion.4, s32[512]{0:T(512)} %param.9, pred[]{:T(512)} %bitcast, pred[]{:T(512)} %bitcast.15, ...), kind=kLoop, calls=%fused_computation.51 | loop fusion | flops 5242880 | bytes 1323013 | tf_op jit(solution)/shard_map/and | solution.py:31
  20.1 5.8 %fusion = (f32[512,2,4]{0,2,1:T(4,128)S(1)}, f32[2,512,512,4]{2,1,3,0:T(8,128)}) fusion(pred[512,512]{0,1:T(8,128)(4,1)S(1)} %get-tuple-element.21, bf16[512,2,4,128]{3,2,1,0:T(4,128)(2,1)S(1)} %reshape.417, bf16[512,2,128,1]{2,1,0,3:T(2,128)(2,1)} %bitcast.161), kind=kOutput, calls=%fused_computation.10 | convolution fusion | flops 543158272 | bytes 9977856 | tf_op jit(solution)/shard_map/tgqd,sgd->tgqs/dot_general | solution.py:25
  26.0 0.0 collective-permute-done.1
  26.0 4.1 %collective-permute-start.3 = (bf16[512,256]{1,0:T(8,128)(2,1)S(1)}, bf16[512,256]{1,0:T(8,128)(2,1)}, u32[]{:S(2)}, u32[]{:S(2)}) collective-permute-start(bf16[512,256]{1,0:T(8,128)(2,1)S(1)} %collective-permute-done.1), channel_id=1, source_target_pairs={{0,4},{4,8},{8,12},{12,16},{16,20},{20,24},{24,28},{1,5},{5,9},{9,... | collective-permute-start | bytes 786440 | tf_op jit(solution)/shard_map/ppermute | solution.py:17
  30.0 0.9 copy.32
  30.9 0.0 collective-permute-done
  30.9 2.8 %collective-permute-start.2 = (bf16[512,256]{0,1:T(8,128)(2,1)S(1)}, bf16[512,256]{0,1:T(8,128)(2,1)S(1)}, u32[]{:S(2)}, u32[]{:S(2)}) collective-permute-start(bf16[512,256]{0,1:T(8,128)(2,1)S(1)} %collective-permute-done), channel_id=1, source_target_pairs={{0,4},{4,8},{8,12},{12,16},{16,20},{20,24},{24,28},{1,5},{5,9},{9,... | collective-permute-start | bytes 786440 | tf_op jit(solution)/shard_map/ppermute | solution.py:17
  33.7 5.0 %fusion.1 = (f32[512,2,4]{0,2,1:T(4,128)S(1)}, f32[2,512,512,4]{2,1,3,0:T(8,128)}) fusion(pred[512,512]{0,1:T(8,128)(4,1)S(1)} %get-tuple-element.25, bf16[512,2,128,1]{0,2,3,1:T(8,128)(2,1)S(1)} %bitcast.155, bf16[512,2,4,128]{3,2,1,0:T(4,128)(2,1)S(1)} %reshape.417), kind=kOutput, calls=%fused_computation.11 | convolution fusion | flops 543158272 | bytes 9977856 | tf_op jit(solution)/shard_map/tgqd,sgd->tgqs/dot_general | solution.py:25
  38.6 0.0 collective-permute-done.3
  38.6 3.4 %collective-permute-start.5 = (bf16[512,256]{1,0:T(8,128)(2,1)}, bf16[512,256]{1,0:T(8,128)(2,1)S(1)}, u32[]{:S(2)}, u32[]{:S(2)}) collective-permute-start(bf16[512,256]{1,0:T(8,128)(2,1)} %collective-permute-done.3), channel_id=1, source_target_pairs={{0,4},{4,8},{8,12},{12,16},{16,20},{20,24},{24,28},{1,5},{5,9},{9,... | collective-permute-start | bytes 786440 | tf_op jit(solution)/shard_map/ppermute | solution.py:17
  42.0 1.8 %copy.36 = bf16[512,256]{0,1:T(8,128)(2,1)} copy(bf16[512,256]{1,0:T(8,128)(2,1)} %collective-permute-done.3) | data formatting | bytes 524288 | tf_op jit(solution)/shard_map/ppermute | solution.py:17
  43.9 0.0 collective-permute-done.2
  43.9 3.4 %collective-permute-start.4 = (bf16[512,256]{0,1:T(8,128)(2,1)S(1)}, bf16[512,256]{0,1:T(8,128)(2,1)S(1)}, u32[]{:S(2)}, u32[]{:S(2)}) collective-permute-start(bf16[512,256]{0,1:T(8,128)(2,1)S(1)} %collective-permute-done.2), channel_id=1, source_target_pairs={{0,4},{4,8},{8,12},{12,16},{16,20},{20,24},{24,28},{1,5},{5,9},{9,... | collective-permute-start | bytes 786440 | tf_op jit(solution)/shard_map/ppermute | solution.py:17
  47.3 5.0 %fusion.2 = (f32[512,2,4]{0,2,1:T(4,128)S(1)}, f32[2,512,512,4]{2,1,3,0:T(8,128)}) fusion(pred[512,512]{0,1:T(8,128)(4,1)S(1)} %get-tuple-element.22, bf16[512,2,128,1]{0,2,3,1:T(8,128)(2,1)S(1)} %bitcast.156, bf16[512,2,4,128]{3,2,1,0:T(4,128)(2,1)S(1)} %reshape.417), kind=kOutput, calls=%fused_computation.12 | convolution fusion | flops 543158272 | bytes 9977856 | tf_op jit(solution)/shard_map/tgqd,sgd->tgqs/dot_general | solution.py:25
  52.3 0.0 collective-permute-done.5
  52.3 4.1 %collective-permute-start.7 = (bf16[512,256]{1,0:T(8,128)(2,1)S(1)}, bf16[512,256]{1,0:T(8,128)(2,1)}, u32[]{:S(2)}, u32[]{:S(2)}) collective-permute-start(bf16[512,256]{1,0:T(8,128)(2,1)S(1)} %collective-permute-done.5), channel_id=1, source_target_pairs={{0,4},{4,8},{8,12},{12,16},{16,20},{20,24},{24,28},{1,5},{5,9},{9,... | collective-permute-start | bytes 786440 | tf_op jit(solution)/shard_map/ppermute | solution.py:17
  56.3 0.8 copy.40
  57.2 0.0 collective-permute-done.4
  57.2 2.3 %collective-permute-start.6 = (bf16[512,256]{0,1:T(8,128)(2,1)S(1)}, bf16[512,256]{0,1:T(8,128)(2,1)S(1)}, u32[]{:S(2)}, u32[]{:S(2)}) collective-permute-start(bf16[512,256]{0,1:T(8,128)(2,1)S(1)} %collective-permute-done.4), channel_id=1, source_target_pairs={{0,4},{4,8},{8,12},{12,16},{16,20},{20,24},{24,28},{1,5},{5,9},{9,... | collective-permute-start | bytes 786440 | tf_op jit(solution)/shard_map/ppermute | solution.py:17
  59.4 0.0 copy-start.3
  59.5 2.2 %fusion.3 = (f32[512,2,4]{0,2,1:T(4,128)S(1)}, f32[2,512,512,4]{2,1,3,0:T(8,128)S(1)}) fusion(pred[512,512]{0,1:T(8,128)(4,1)S(1)} %get-tuple-element.23, bf16[512,2,128,1]{0,2,3,1:T(8,128)(2,1)S(1)} %bitcast.157, bf16[512,2,4,128]{3,2,1,0:T(4,128)(2,1)S(1)} %reshape.417), kind=kOutput, calls=%fused_computation.13 | convolution fusion | flops 543158272 | bytes 9977856 | tf_op jit(solution)/shard_map/tgqd,sgd->tgqs/dot_general | solution.py:25
  61.6 3.5 %collective-permute-done.6 = bf16[512,256]{0,1:T(8,128)(2,1)S(1)} collective-permute-done((bf16[512,256]{0,1:T(8,128)(2,1)S(1)}, bf16[512,256]{0,1:T(8,128)(2,1)S(1)}, u32[]{:S(2)}, u32[]{:S(2)}) %collective-permute-start.6) | collective-permute-done | bytes 262176 | tf_op jit(solution)/shard_map/ppermute | solution.py:17
  65.1 2.2 %fusion.4 = (f32[512,2,4]{0,2,1:T(4,128)S(1)}, f32[2,512,512,4]{2,1,3,0:T(8,128)S(1)}) fusion(pred[512,512]{0,1:T(8,128)(4,1)S(1)} %get-tuple-element.24, bf16[512,2,128,1]{0,2,3,1:T(8,128)(2,1)S(1)} %bitcast.158, bf16[512,2,4,128]{3,2,1,0:T(4,128)(2,1)S(1)} %reshape.417), kind=kOutput, calls=%fused_computation.14 | convolution fusion | flops 543158272 | bytes 9977856 | tf_op jit(solution)/shard_map/tgqd,sgd->tgqs/dot_general | solution.py:25
  67.3 0.0 slice-start.2
  67.4 0.0 slice-start.3
  67.4 4.0 %fusion.17 = f32[2,512,4,128]{1,3,2,0:T(8,128)} fusion(bf16[512,2,128,1]{0,2,3,1:T(8,128)(2,1)S(1)} %bitcast.163, f32[2,512,512,4]{2,1,3,0:T(8,128)S(1)} %get-tuple-element.29, f32[512,2,4]{0,2,1:T(4,128)S(1)} %get-tuple-element.14, pred[512,512]{0,1:T(8,128)(4,1)S(1)} %get-tuple-element.23), kind=kOutput, calls=%fused_computation.26 | convolution fusion | flops 547356672 | bytes 11026432 | tf_op jit(solution)/shard_map/tgqs,sgd->tgqd/dot_general | solution.py:42
  71.4 1.2 slice-done.2
  72.6 1.9 %slice-done.3 = s8[4194304]{0:T(1024)(128)(4,1)S(1)} async-done(((s8[8388608]{0:T(1024)(128)(4,1)}), s8[4194304]{0:T(1024)(128)(4,1)S(1)}, s32[]{:S(2)}) %slice-start.3) | async-done | bytes 4194328
  74.5 4.0 %fusion.9 = (f32[512,2,4]{0,2,1:T(4,128)S(1)}, f32[512,2,4]{0,2,1:T(4,128)S(1)}) fusion(f32[2,512,512,4]{2,1,3,0:T(8,128)S(1)} %bitcast.151, f32[512,2,4]{0,2,1:T(4,128)S(1)} %get-tuple-element.15, pred[512,512]{0,1:T(8,128)(4,1)S(1)} %get-tuple-element.22, f32[512,2,4]{0,2,1:T(4,128)S(1)} %get-tuple-element.14, ...), kind=kLoop, calls=%fused_computation.19 | loop fusion | flops 20963328 | bytes 17367040 | tf_op jit(solution)/shard_map/reduce_sum | solution.py:40
  78.6 4.1 %fusion.19 = f32[2,512,4,128]{1,3,2,0:T(8,128)} fusion(bf16[512,2,128,1]{0,2,3,1:T(8,128)(2,1)S(1)} %bitcast.162, f32[2,512,512,4]{2,1,3,0:T(8,128)S(1)} %bitcast.151, f32[512,2,4]{0,2,1:T(4,128)S(1)} %get-tuple-element.15, pred[512,512]{0,1:T(8,128)(4,1)S(1)} %get-tuple-element.22), kind=kOutput, calls=%fused_computation.27 | convolution fusion | flops 547356672 | bytes 11026432 | tf_op jit(solution)/shard_map/tgqs,sgd->tgqd/dot_general | solution.py:42
  82.7 0.0 slice-start.5
  82.7 4.0 %fusion.21 = f32[2,512,4,128]{1,3,2,0:T(8,128)} fusion(bf16[512,2,128,1]{0,2,3,1:T(8,128)(2,1)S(1)} %bitcast.160, f32[2,512,512,4]{2,1,3,0:T(8,128)S(1)} %bitcast.149, f32[512,2,4]{0,2,1:T(4,128)S(1)} %get-tuple-element.16, pred[512,512]{0,1:T(8,128)(4,1)S(1)} %get-tuple-element.25), kind=kOutput, calls=%fused_computation.28 | convolution fusion | flops 547356672 | bytes 11026432 | tf_op jit(solution)/shard_map/tgqs,sgd->tgqd/dot_general | solution.py:42
  86.7 4.3 %fusion.5 = (f32[512,2,4]{0,2,1:T(4,128)S(1)}, f32[512,2,4]{0,2,1:T(4,128)S(1)}) fusion(f32[2,512,512,4]{2,1,3,0:T(8,128)S(1)} %bitcast.153, f32[512,2,4]{0,2,1:T(4,128)S(1)} %get-tuple-element.20, pred[512,512]{0,1:T(8,128)(4,1)S(1)} %get-tuple-element.21, f32[512,2,4]{0,2,1:T(4,128)S(1)} %get-tuple-element.16, f32[2,512,512,4]{2,1,3,0:T(8,128)S(1)} %bitcast.149, ...), kind=kLoop, calls=%fused_computation.15 | loop fusion | flops 20963328 | bytes 17367040 | tf_op jit(solution)/shard_map/reduce_sum | solution.py:40
  91.0 4.1 %fusion.23 = f32[2,512,4,128]{1,3,2,0:T(8,128)} fusion(bf16[512,2,128,1]{0,2,3,1:T(8,128)(2,1)S(1)} %bitcast.159, f32[2,512,512,4]{2,1,3,0:T(8,128)S(1)} %bitcast.153, f32[512,2,4]{0,2,1:T(4,128)S(1)} %get-tuple-element.20, pred[512,512]{0,1:T(8,128)(4,1)S(1)} %get-tuple-element.21), kind=kOutput, calls=%fused_computation.29 | convolution fusion | flops 547356672 | bytes 11026432 | tf_op jit(solution)/shard_map/tgqs,sgd->tgqd/dot_general | solution.py:42
  95.1 2.0 %fusion.13 = f32[512,2,4]{0,2,1:T(4,128)S(1)} fusion(f32[2,512,512,4]{2,1,3,0:T(8,128)S(1)} %get-tuple-element.27, f32[512,2,4]{0,2,1:T(4,128)S(1)} %get-tuple-element.13, pred[512,512]{0,1:T(8,128)(4,1)S(1)} %get-tuple-element.24), kind=kLoop, calls=%fused_computation.23 | loop fusion | flops 10481664 | bytes 8683520 | tf_op jit(solution)/shard_map/reduce_sum | solution.py:40
  97.1 0.1 multiply_add_fusion
  97.2 1.1 copy.44
  98.2 9.7 %fusion.30 = (f32[]{:T(128)}, bf16[512,2,4,128]{0,3,2,1:T(8,128)(2,1)S(1)}) fusion(f32[512]{0:T(512)S(1)} %convert_element_type.31, f32[512,2,4]{0,2,1:T(4,128)S(1)} %get-tuple-element.8, bf16[512,2,128,1]{0,2,3,1:T(8,128)(2,1)S(1)} %bitcast.164, f32[2,512,512,4]{2,1,3,0:T(8,128)} %copy-done, f32[512,2,4]{0,2,1:T(4,128)S(1)} %get-tuple-element.13, ...), kind=kOutput, calls=%fused_computation.36 | convolution fusion | flops 554696704 | bytes 18466820 | tf_op jit(solution)/shard_map/tgqs,sgd->tgqd/dot_general | solution.py:42
  108.0 1.3 copy.46
  109.3 40.6 %all-reduce = (f32[]{:T(128)}, f32[]{:T(128)}) all-reduce(f32[]{:T(128)} %get-tuple-element.17, f32[]{:T(128)S(6)} %select_n.45), channel_id=1, replica_groups=mesh['seq'=8,'head'=4] {'seq','head'}, use_global_device_ids=true, to_apply=%region_11.12 | all-reduce | flops 2 | bytes 16 | tf_op jit(solution)/shard_map/psum | solution.py:86
  (24 shorter events, 0.1 us)
Async XLA Ops:
  1.7 29.2 %collective-permute-start = (bf16[512,256]{0,1:T(8,128)(2,1)S(1)}, bf16[512,256]{0,1:T(8,128)(2,1)S(1)}, u32[]{:S(2)}, u32[]{:S(2)}) collective-permute-start(bf16[512,256]{0,1:T(8,128)(2,1)S(1)} %copy.29), channel_id=1, source_target_pairs={{0,4},{4,8},{8,12},{12,16},{16,20},{20,24},{24,28},{1,5},{5,9},{9,... | collective-permute-start | bytes 786440 | tf_op jit(solution)/shard_map/ppermute | solution.py:17
  6.6 19.3 %collective-permute-start.1 = (bf16[512,256]{1,0:T(8,128)(2,1)}, bf16[512,256]{1,0:T(8,128)(2,1)S(1)}, u32[]{:S(2)}, u32[]{:S(2)}) collective-permute-start(bf16[512,256]{1,0:T(8,128)(2,1)} %param.8), channel_id=1, source_target_pairs={{0,4},{4,8},{8,12},{12,16},{16,20},{20,24},{24,28},{1,5},{5,9},{9,... | collective-permute-start | bytes 786440 | tf_op jit(solution)/shard_map/ppermute | solution.py:17
  26.0 12.7 %collective-permute-start.3 = (bf16[512,256]{1,0:T(8,128)(2,1)S(1)}, bf16[512,256]{1,0:T(8,128)(2,1)}, u32[]{:S(2)}, u32[]{:S(2)}) collective-permute-start(bf16[512,256]{1,0:T(8,128)(2,1)S(1)} %collective-permute-done.1), channel_id=1, source_target_pairs={{0,4},{4,8},{8,12},{12,16},{16,20},{20,24},{24,28},{1,5},{5,9},{9,... | collective-permute-start | bytes 786440 | tf_op jit(solution)/shard_map/ppermute | solution.py:17
  30.9 13.0 %collective-permute-start.2 = (bf16[512,256]{0,1:T(8,128)(2,1)S(1)}, bf16[512,256]{0,1:T(8,128)(2,1)S(1)}, u32[]{:S(2)}, u32[]{:S(2)}) collective-permute-start(bf16[512,256]{0,1:T(8,128)(2,1)S(1)} %collective-permute-done), channel_id=1, source_target_pairs={{0,4},{4,8},{8,12},{12,16},{16,20},{20,24},{24,28},{1,5},{5,9},{9,... | collective-permute-start | bytes 786440 | tf_op jit(solution)/shard_map/ppermute | solution.py:17
  38.6 13.6 %collective-permute-start.5 = (bf16[512,256]{1,0:T(8,128)(2,1)}, bf16[512,256]{1,0:T(8,128)(2,1)S(1)}, u32[]{:S(2)}, u32[]{:S(2)}) collective-permute-start(bf16[512,256]{1,0:T(8,128)(2,1)} %collective-permute-done.3), channel_id=1, source_target_pairs={{0,4},{4,8},{8,12},{12,16},{16,20},{20,24},{24,28},{1,5},{5,9},{9,... | collective-permute-start | bytes 786440 | tf_op jit(solution)/shard_map/ppermute | solution.py:17
  43.9 13.3 %collective-permute-start.4 = (bf16[512,256]{0,1:T(8,128)(2,1)S(1)}, bf16[512,256]{0,1:T(8,128)(2,1)S(1)}, u32[]{:S(2)}, u32[]{:S(2)}) collective-permute-start(bf16[512,256]{0,1:T(8,128)(2,1)S(1)} %collective-permute-done.2), channel_id=1, source_target_pairs={{0,4},{4,8},{8,12},{12,16},{16,20},{20,24},{24,28},{1,5},{5,9},{9,... | collective-permute-start | bytes 786440 | tf_op jit(solution)/shard_map/ppermute | solution.py:17
  52.3 44.9 %collective-permute-start.7 = (bf16[512,256]{1,0:T(8,128)(2,1)S(1)}, bf16[512,256]{1,0:T(8,128)(2,1)}, u32[]{:S(2)}, u32[]{:S(2)}) collective-permute-start(bf16[512,256]{1,0:T(8,128)(2,1)S(1)} %collective-permute-done.5), channel_id=1, source_target_pairs={{0,4},{4,8},{8,12},{12,16},{16,20},{20,24},{24,28},{1,5},{5,9},{9,... | collective-permute-start | bytes 786440 | tf_op jit(solution)/shard_map/ppermute | solution.py:17
  57.2 8.0 %collective-permute-start.6 = (bf16[512,256]{0,1:T(8,128)(2,1)S(1)}, bf16[512,256]{0,1:T(8,128)(2,1)S(1)}, u32[]{:S(2)}, u32[]{:S(2)}) collective-permute-start(bf16[512,256]{0,1:T(8,128)(2,1)S(1)} %collective-permute-done.4), channel_id=1, source_target_pairs={{0,4},{4,8},{8,12},{12,16},{16,20},{20,24},{24,28},{1,5},{5,9},{9,... | collective-permute-start | bytes 786440 | tf_op jit(solution)/shard_map/ppermute | solution.py:17
  59.4 7.9 %copy-start.3 = (bf16[512,256]{0,1:T(8,128)(2,1)S(1)}, bf16[512,256]{0,1:T(8,128)(2,1)}, u32[]{:S(2)}) copy-start(bf16[512,256]{0,1:T(8,128)(2,1)} %copy.40) | copy-start | bytes 786436
  67.3 27.7 %copy-start = (f32[2,512,512,4]{2,1,3,0:T(8,128)}, f32[2,512,512,4]{2,1,3,0:T(8,128)S(1)}, u32[]{:S(2)}) copy-start(f32[2,512,512,4]{2,1,3,0:T(8,128)S(1)} %get-tuple-element.27) | copy-start | bytes 25165828
  67.3 5.3 %slice-start.2 = ((s8[8388608]{0:T(1024)(128)(4,1)}), s8[4194304]{0:T(1024)(128)(4,1)S(1)}, s32[]{:S(2)}) async-start(s8[8388608]{0:T(1024)(128)(4,1)} %bitcast.150), calls=%async_computation.2 | async-start | bytes 8388608
  67.4 7.1 %slice-start.3 = ((s8[8388608]{0:T(1024)(128)(4,1)}), s8[4194304]{0:T(1024)(128)(4,1)S(1)}, s32[]{:S(2)}) async-start(s8[8388608]{0:T(1024)(128)(4,1)} %bitcast.150), calls=%async_computation.3 | async-start | bytes 8388608
  74.5 4.1 %copy-start.2 = (bf16[512,256]{0,1:T(8,128)(2,1)S(1)}, bf16[512,256]{0,1:T(8,128)(2,1)}, u32[]{:S(2)}) copy-start(bf16[512,256]{0,1:T(8,128)(2,1)} %copy.36) | copy-start | bytes 786436
  78.5 4.1 %slice-start = ((s8[8388608]{0:T(1024)(128)(4,1)}), s8[4194304]{0:T(1024)(128)(4,1)S(1)}, s32[]{:S(2)}) async-start(s8[8388608]{0:T(1024)(128)(4,1)} %bitcast.148), calls=%async_computation | async-start | bytes 8388608
  78.6 4.1 %copy-start.1 = (bf16[512,256]{0,1:T(8,128)(2,1)S(1)}, bf16[512,256]{0,1:T(8,128)(2,1)}, u32[]{:S(2)}) copy-start(bf16[512,256]{0,1:T(8,128)(2,1)} %copy.32) | copy-start | bytes 786436
  78.6 4.1 %slice-start.1 = ((s8[8388608]{0:T(1024)(128)(4,1)}), s8[4194304]{0:T(1024)(128)(4,1)S(1)}, s32[]{:S(2)}) async-start(s8[8388608]{0:T(1024)(128)(4,1)} %bitcast.148), calls=%async_computation.1 | async-start | bytes 8388608
  82.7 4.0 %slice-start.4 = ((s8[8388608]{0:T(1024)(128)(4,1)}), s8[4194304]{0:T(1024)(128)(4,1)S(1)}, s32[]{:S(2)}) async-start(s8[8388608]{0:T(1024)(128)(4,1)} %bitcast.152), calls=%async_computation.4 | async-start | bytes 8388608
  82.7 4.0 %slice-start.5 = ((s8[8388608]{0:T(1024)(128)(4,1)}), s8[4194304]{0:T(1024)(128)(4,1)S(1)}, s32[]{:S(2)}) async-start(s8[8388608]{0:T(1024)(128)(4,1)} %bitcast.152), calls=%async_computation.5 | async-start | bytes 8388608
where the time goes:
time: 153 us; the launch traced here: 152 us
  matrix products  45.9 us (30%)
  blocking collectives  40.6 us (27%)
  starting transfers between devices  28.3 us (18%)
  local copies, waits for them, and re-layouts  14.8 us (10%)
  other arithmetic  14.5 us (9%)
  between operations  4.68 us (3%)
  waiting for transfers between devices  3.52 us (2%)
    psum x1, blocking collectives, on_device(): lax.psum((local_squares, share), ('seq', 'head'))  40.6 us
    ppermute x8, starting transfers between devices, passed_along(): return lax.ppermute(shard, axis, pairs)  28.3 us
    dot_general x5, matrix products, attend_block(): jnp.einsum('tgqs,sgd->tgqd', rounded, value_block, preferred_element_type...  25.8 us
    dot_general x5, matrix products, attend_block(): jnp.einsum('tgqd,sgd->tgqs', grouped_queries, key_block, preferred_elemen...  20.1 us
    reduce_sum x3, other arithmetic, attend_block(): total_new = total_old * ratio_old + jnp.sum(weights, axis=-1)  10.4 us
    unnamed x22, local copies, waits for them, and re-layouts  5.54 us
    ppermute x4, local copies, waits for them, and re-layouts, passed_along(): return lax.ppermute(shard, axis, pairs)  4.63 us
    ppermute x8, waiting for transfers between devices, passed_along(): return lax.ppermute(shard, axis, pairs)  3.52 us
  transfers between devices with their start and end apart: 8, of which 1 were waited for; matrix products, arithmetic and copies ran while one was open for 39% of the time, Pallas kernels for 0%

commit v1 on v0

v1 whole, which is shorter than its diff:
```python
import functools
import math

import jax
import jax.numpy as jnp
from jax import lax
from jax.experimental import pallas as pl
from jax.experimental.pallas import tpu as pltpu
from jax.sharding import PartitionSpec as P

QUERY_HEADS = 32
KEY_VALUE_HEADS = 8
HEAD_WIDTH = 128
HOPS = 4

MESH = pl.DeviceIdType.MESH
CHUNK = 64
STEP = 256
DOCUMENT = 2048
LOW = -1e30

Z1, Z2, X1, X2 = range(4)
DISTANCE = {Z1: 2, Z2: 4, X1: 1, X2: 3}


def kernel(
    blocks, groups, q_ref, k_ref, v_ref, start_ref, hop_ref, mask_ref, out_ref, obj_ref,
    got_k, got_v, acc, top, first, marks, bias, joined, stat, stat_got, row, row_got,
    send_z, send_x, recv, send_s, recv_s, send_r, recv_r,
):
    rows = q_ref.shape[0]
    heads = q_ref.shape[1] // HEAD_WIDTH
    group_size = QUERY_HEADS // KEY_VALUE_HEADS
    chunks = rows // CHUNK
    per_step = STEP // CHUNK
    scale = math.log2(math.e) / math.sqrt(HEAD_WIDTH)
    b = lax.axis_index("seq")
    hd = lax.axis_index("head")
    odd = lax.rem(b, 2)
    partner = b + 1 - 2 * odd

    barrier = pltpu.get_barrier_semaphore()
    for k in range(1, groups):
        pl.semaphore_signal(
            barrier, inc=1, device_id=(b, lax.rem(hd + k, groups)), device_id_type=MESH
        )

    def greet(k, carry):
        pl.semaphore_signal(
            barrier, inc=1, device_id=(lax.rem(b + k, blocks), hd), device_id_type=MESH
        )
        return carry

    lax.fori_loop(1, blocks, greet, 0)
    pl.semaphore_wait(barrier, blocks + groups - 2)

    def pair(src_k, src_v, slot, c, send, to):
        at = pl.ds(c * CHUNK, CHUNK)
        made = []
        for which, (src, dst) in enumerate(((src_k, got_k), (src_v, got_v))):
            made.append(
                pltpu.make_async_remote_copy(
                    src_ref=src.at[at, :],
                    dst_ref=dst.at[slot, at, :],
                    send_sem=send.at[which],
                    recv_sem=recv.at[slot, c, which],
                    device_id=(to, hd),
                    device_id_type=MESH,
                )
            )
        return made

    up = b + 2
    has_up = up < blocks

    def own_z(c):
        return pair(k_ref, v_ref, Z1, c, send_z.at[0, c], up)

    def on_z(c):
        return pair(got_k.at[Z1], got_v.at[Z1], Z2, c, send_z.at[1, c], up)

    def even_first(c):
        return pair(k_ref, v_ref, X1, c, send_x.at[0, c], partner)

    def even_second(c):
        return pair(got_k.at[Z1], got_v.at[Z1], X2, c, send_x.at[1, c], partner)

    def odd_first(c):
        return pair(got_k.at[Z1], got_v.at[Z1], X1, c, send_x.at[0, c], partner)

    def odd_second(c):
        return pair(got_k.at[Z2], got_v.at[Z2], X2, c, send_x.at[1, c], partner)

    def begin(copies):
        for copy in copies:
            copy.start()

    def sent(copies):
        for copy in copies:
            copy.wait_send()

    def landed(slot, c):
        for copy in pair(k_ref, v_ref, slot, c, send_z.at[0, c], partner):
            copy.wait_recv()

    for c in range(chunks):
        @pl.when(has_up)
        def _():
            begin(own_z(c))

        @pl.when(odd == 0)
        def _():
            begin(even_first(c))

    def column(line):
        return jnp.broadcast_to(line.astype(jnp.float32), (HEAD_WIDTH, rows)).T

    first[...] = column(jnp.maximum(start_ref[...], (b - hop_ref[0]) * rows))
    marks[...] = column(mask_ref[...])
    joined[...] = jnp.ones_like(joined)

    def attend(keys, values, offset, distance, fresh=False):
        base = (b - distance) * rows + offset
        at = pl.ds(offset, STEP)
        lo = offset if distance == 0 else 0
        hi = max(0, min(rows, DOCUMENT + offset + STEP - 1 - distance * rows))
        lo, hi = lo // 128 * 128, min(rows, -(-hi // 128) * 128)
        span = slice(lo, hi)
        tile = (hi - lo, 128)
        for j in range(0, STEP, 128):
            spot = base + j + lax.broadcasted_iota(jnp.int32, tile, 1)
            seen = spot.astype(jnp.float32) >= first[span]
            if distance == 0:
                seen = seen & (spot <= b * rows + lo + lax.broadcasted_iota(jnp.int32, tile, 0))
            bias[span, j : j + 128] = jnp.where(seen, 0.0, LOW)
        for g in range(heads // group_size):
            joined[g, :, :HEAD_WIDTH] = values[at, g * HEAD_WIDTH : (g + 1) * HEAD_WIDTH]

        def one(h, g):
            lanes = pl.ds(pl.multiple_of(h * HEAD_WIDTH, HEAD_WIDTH), HEAD_WIDTH)
            kv = pl.ds(g * HEAD_WIDTH, HEAD_WIDTH)
            s = lax.dot_general(
                q_ref[span, lanes], keys[at, kv], (((1,), (1,)), ((), ())),
                preferred_element_type=jnp.float32,
            ) + bias[span]
            new = jnp.broadcast_to(jnp.max(s, axis=1, keepdims=True), tile)
            if not fresh:
                old = top[h, span]
                new = jnp.maximum(old, new)
            p = jnp.concatenate(
                [
                    jnp.exp2((s[:, j : j + 128] - new) * scale).astype(jnp.bfloat16)
                    for j in range(0, STEP, 128)
                ],
                axis=1,
            )
            update = jnp.dot(p, joined[g], preferred_element_type=jnp.float32)
            top[h, span] = new
            if not fresh:
                ratio = jnp.exp2((old - new) * scale)
                update = acc[h, span] * jnp.concatenate([ratio, ratio], axis=1) + update
            acc[h, span] = update

        def body(i, carry):
            for g in range(heads // group_size):
                one(g * group_size + i, g)
            return carry

        lax.fori_loop(0, group_size, body, 0)

    def take(slot, c):
        @pl.when(b >= DISTANCE[slot])
        def _():
            landed(slot, c)
            if slot == Z1:
                @pl.when(has_up)
                def _():
                    begin(on_z(c))

                @pl.when(odd == 0)
                def _():
                    begin(even_second(c))

                @pl.when(odd == 1)
                def _():
                    begin(odd_first(c))
            if slot == Z2:
                @pl.when(odd == 1)
                def _():
                    begin(odd_second(c))

    def work(slot, step):
        @pl.when(b >= DISTANCE[slot])
        def _():
            attend(got_k.at[slot], got_v.at[slot], step * STEP, DISTANCE[slot])

    steps = rows // STEP
    for step in range(steps):
        attend(k_ref, v_ref, step * STEP, 0, fresh=step == 0)

    for step in range(steps):
        for c in range(step * per_step, (step + 1) * per_step):
            take(Z1, c)
        work(Z1, step)
    pending = []
    for step in range(steps):
        pending.append((X1, step))
    for c in range(chunks):
        take(Z2, c)
        if c % per_step == per_step // 2 - 1 and pending:
            slot, step = pending.pop(0)
            for d in range(step * per_step, (step + 1) * per_step):
                take(slot, d)
            work(slot, step)
        if c % per_step == per_step - 1:
            step = c // per_step
            if step < steps - 1:
                work(Z2, step)
                for d in range(step * per_step, (step + 1) * per_step):
                    take(X2, d)
                work(X2, step)
            else:
                work(Z2, step)
    for slot, step in pending:
        for d in range(step * per_step, (step + 1) * per_step):
            take(slot, d)
        work(slot, step)
    last = steps - 1
    for d in range(last * per_step, (last + 1) * per_step):
        take(X2, d)
    work(X2, last)

    def finish(h):
        attended = acc[h, :, :HEAD_WIDTH] * (1.0 / acc[h, :, HEAD_WIDTH:])
        out_ref[:, h * HEAD_WIDTH : (h + 1) * HEAD_WIDTH] = attended.astype(jnp.bfloat16)
        return jnp.sum((attended * attended * marks[...]).reshape(rows // 8, 8, 128), axis=0)

    squares = finish(0)
    for h in range(1, heads):
        squares = squares + finish(h)
    stat[:8] = squares
    stat[8:] = jnp.sum(marks[...].reshape(rows // 8, 8, 128), axis=0)

    def to_head(k):
        return pltpu.make_async_remote_copy(
            src_ref=stat, dst_ref=stat_got.at[k], send_sem=send_s.at[k], recv_sem=recv_s.at[k],
            device_id=(b, lax.rem(hd + k, groups)), device_id_type=MESH,
        )

    def to_block(k):
        return pltpu.make_async_remote_copy(
            src_ref=row, dst_ref=row_got.at[k], send_sem=send_r.at[k], recv_sem=recv_r.at[k],
            device_id=(lax.rem(b + k, blocks), hd), device_id_type=MESH,
        )

    for c in range(chunks):
        @pl.when(has_up)
        def _():
            sent(own_z(c))

            @pl.when(b >= DISTANCE[Z1])
            def _():
                sent(on_z(c))

        @pl.when(odd == 0)
        def _():
            sent(even_first(c))

            @pl.when(b >= DISTANCE[Z1])
            def _():
                sent(even_second(c))

        @pl.when((odd == 1) & (b >= DISTANCE[Z1]))
        def _():
            sent(odd_first(c))

        @pl.when((odd == 1) & (b >= DISTANCE[Z2]))
        def _():
            sent(odd_second(c))
    for k in range(1, groups):
        to_head(k).start()
    whole = stat[...]
    for k in range(1, groups):
        to_head(k).wait_recv()
        whole = whole + stat_got[k]
    row[...] = whole
    for k in range(1, groups):
        to_head(k).wait_send()

    def give(k, carry):
        to_block(k).start()
        return carry

    lax.fori_loop(1, blocks, give, 0)


    def gather(k, so_far):
        to_block(k).wait()
        return so_far + row_got[k]

    final = lax.fori_loop(1, blocks, gather, row[...])
    square_sum = jnp.sum(final[:8], keepdims=True)
    count = jnp.sum(final[8:], keepdims=True) * (1.0 / (groups * 128))
    obj_ref[...] = jnp.broadcast_to(square_sum / (QUERY_HEADS * count), obj_ref.shape)


def solution(mesh):
    blocks, groups = mesh.shape["seq"], mesh.shape["head"]

    def on_device(queries, keys, values, doc_start, hop_counts, loss_mask):
        rows, width = queries.shape
        heads = width // HEAD_WIDTH
        chunks = rows // CHUNK
        vmem = pl.BlockSpec(memory_space=pltpu.VMEM)
        dma = pltpu.SemaphoreType.DMA
        attention, objective = pl.pallas_call(
            functools.partial(kernel, blocks, groups),
            out_shape=(
                jax.ShapeDtypeStruct((rows, width), jnp.bfloat16),
                jax.ShapeDtypeStruct((1, 128), jnp.float32),
            ),
            in_specs=[vmem] * 4 + [pl.BlockSpec(memory_space=pltpu.SMEM), vmem],
            out_specs=(vmem, vmem),
            scratch_shapes=[
                pltpu.VMEM((4, *keys.shape), jnp.bfloat16),
                pltpu.VMEM((4, *values.shape), jnp.bfloat16),
                pltpu.VMEM((heads, rows, 2 * HEAD_WIDTH), jnp.float32),
                pltpu.VMEM((heads, rows, 128), jnp.float32),
                pltpu.VMEM((rows, 128), jnp.float32),
                pltpu.VMEM((rows, 128), jnp.float32),
                pltpu.VMEM((rows, STEP), jnp.float32),
                pltpu.VMEM((keys.shape[1] // HEAD_WIDTH, STEP, 2 * HEAD_WIDTH), jnp.bfloat16),
                pltpu.VMEM((16, 128), jnp.float32),
                pltpu.VMEM((groups, 16, 128), jnp.float32),
                pltpu.VMEM((16, 128), jnp.float32),
                pltpu.VMEM((blocks, 16, 128), jnp.float32),
                dma((2, chunks, 2)),
                dma((2, chunks, 2)),
                dma((4, chunks, 2)),
                dma((groups,)),
                dma((groups,)),
                dma((blocks,)),
                dma((blocks,)),
            ],
            compiler_params=pltpu.CompilerParams(collective_id=0, has_side_effects=True),
        )(
            queries, keys, values, doc_start.reshape(1, rows), hop_counts,
            loss_mask.reshape(1, rows),
        )
        return attention, objective[0, 0]

    placed = (P("seq", "head"), P("seq", "head"), P("seq", "head"), P("seq"), P("seq"), P("seq"))
    return jax.shard_map(
        on_device, mesh=mesh, in_specs=placed, out_specs=(P("seq", "head"), P()), check_vma=False
    )
```

time: 153 us -> 54.9 us (0.36)
  Pallas kernels: 0 us -> 50 us
  matrix products: 45.9 us -> 0 us
  blocking collectives: 40.6 us -> 0 us
  starting transfers between devices: 28.3 us -> 0 us
  other arithmetic: 14.5 us -> 0 us
  local copies, waits for them, and re-layouts: 14.8 us -> 2.27 us
  waiting for transfers between devices: 3.52 us -> 0 us
  between operations: 4.68 us -> 2.46 us
    pallas_call x0 -> x1, Pallas kernels: none -> 50 us  [on_device(): pl.pallas_call(functools.partial(kernel, blocks, groups), out_shape=(jax....]
    dot_general x10 -> x0, matrix products: 45.9 us -> none  [the longest x5 25.8 us: attend_block(): jnp.einsum('tgqs,sgd->tgqd', rounded, value_block, preferred_element_type...]
    psum x1 -> x0, blocking collectives: 40.6 us -> none  [on_device(): lax.psum((local_squares, share), ('seq', 'head'))]
    ppermute x8 -> x0, starting transfers between devices: 28.3 us -> none  [passed_along(): return lax.ppermute(shard, axis, pairs)]
    reduce_sum x4 -> x0, other arithmetic: 11.7 us -> none  [the longest x3 10.4 us: attend_block(): total_new = total_old * ratio_old + jnp.sum(weights, axis=-1)]
    ppermute x4 -> x0, local copies, waits for them, and re-layouts: 4.63 us -> none  [passed_along(): return lax.ppermute(shard, axis, pairs)]
    reshape x3 -> x0, local copies, waits for them, and re-layouts: 4.6 us -> none  [the longest x1 1.79 us: on_device(): grouped_queries = queries.reshape(rows, kv_heads, group_size, HEAD_WIDTH)]
    ppermute x8 -> x0, waiting for transfers between devices: 3.52 us -> none  [passed_along(): return lax.ppermute(shard, axis, pairs)]
  transfers between devices with their start and end apart: 8 -> 0, of which waited for: 1 -> 0; matrix products, arithmetic and copies ran while one was open for 39% -> 0% of each run, Pallas kernels for 0% -> 0%
where the time goes in v1:
time: 54.9 us; the launch traced here: 54.7 us
  Pallas kernels  50 us (91%)
  between operations  2.46 us (4%)
  local copies, waits for them, and re-layouts  2.27 us (4%)
    pallas_call x1, Pallas kernels, on_device(): pl.pallas_call(functools.partial(kernel, blocks, groups), out_shape=(jax....  50 us
    unnamed x3, local copies, waits for them, and re-layouts  2.27 us

profile of v1, /device:TPU:0, one launch (start us, length us, event | category | flops | bytes accessed | tf_op | source)
XLA Modules:
  0.0 54.7 jit_solution(12710736995723434233)
XLA Ops:
  1.3 50.0 %shard_map.77 = (bf16[512,1024]{1,0:T(8,128)(2,1)}, f32[1,128]{1,0:T(1,128)}) custom-call(bf16[512,1024]{1,0:T(8,128)(2,1)} %q_ref.1, bf16[512,256]{1,0:T(8,128)(2,1)} %k_ref.1, bf16[512,256]{1,0:T(8,128)(2,1)} %v_ref.1, s32[1,512]{1,0:T(1,128)} %bitcast.4, s32[1]{0:T(128)S(6)} %copy.10.hop_ref, s32[1,512]{1,0:T(1,128)} %bitcast.5), custom_call_target="tpu_custom_call" | custom-call | tf_op jit(solution)/shard_map/pallas_call | solution.py:316
  51.2 0.0 copy-start
  51.2 2.3 %copy.11 = bf16[512,1024]{1,0:T(8,128)(2,1)} copy(bf16[512,1024]{1,0:T(8,128)(2,1)} %get-tuple-element.8) | data formatting | bytes 2097152
  53.5 0.0 copy-done
Async XLA Ops:
  51.2 2.3 %copy-start = (f32[1,128]{1,0:T(1,128)S(1)}, f32[1,128]{1,0:T(1,128)}, u32[]{:S(2)}) copy-start(f32[1,128]{1,0:T(1,128)} %get-tuple-element.5) | copy-start | bytes 1540
